TPU v7x, 256 devices: a whole 4x4x8 slice. The times are simulated.
256 devices in a mesh: dp: 32 (over y, x, core), mp: 8 (over z).
Axes of the slice: x: 4, y: 4, z: 8, core: 2. Of those that a mesh axis runs over, the one named last changes fastest.
Arguments:
- clean: bfloat16 [128, 256, 1536], P('dp', None, 'mp'), may hold values from -6 to 6
- noise: bfloat16 [128, 256, 1536], P('dp', None, 'mp'), may hold values from -6 to 6
- teacher_first: bfloat16 [128, 256, 1536], P('dp', None, 'mp'), may hold values from -6 to 6
- teacher_second: bfloat16 [128, 256, 1536], P('dp', None, 'mp'), may hold values from -6 to 6
- step_index: int32 [128], P('dp'), may hold values from 8 to 32
- teacher_count: int32 [128], P('dp'), may hold values from 64 to 256
- up_master: float32 [1536, 6144], P('dp', 'mp'), may hold values from -6 to 6
- down_master: float32 [1536, 6144], P('dp', 'mp'), may hold values from -6 to 6
- up_moment: float32 [1536, 6144], P('dp', 'mp'), may hold values from -1.8 to 1.8
- down_moment: float32 [1536, 6144], P('dp', 'mp'), may hold values from -1.8 to 1.8
- up_second: float32 [1536, 6144], P('dp', 'mp'), may hold values from 0.002 to 0.032
- down_second: float32 [1536, 6144], P('dp', 'mp'), may hold values from 0.002 to 0.032
Outputs:
- new_up_master: float32 [1536, 6144], P('dp', 'mp')
- new_down_master: float32 [1536, 6144], P('dp', 'mp')
- new_up_moment: float32 [1536, 6144], P('dp', 'mp')
- new_down_moment: float32 [1536, 6144], P('dp', 'mp')
- new_up_second: float32 [1536, 6144], P('dp', 'mp')
- new_down_second: float32 [1536, 6144], P('dp', 'mp')
- loss_mean: float32 [], replicated
Inputs may be any that keep to these rules, and one draw needn't show every extreme that they name: `step_index`: student step k with 2k at most the sample's teacher_count.
All inputs are finite; a program needn't handle non-finite values.
Results may differ from a plain program's by a relative error of at most 0.002.
Values may be sent and summed in bfloat16 or wider, within the bound.
No kernel may reach another device: no remote copies, remote signals or barrier semaphores. Data moves between devices by JAX's collectives and lax.ppermute only.
A program may use at most 64 MiB of HBM per device.

v0:
```python
import functools
import math
import jax
import jax.numpy as jnp
from jax import lax
from jax.sharding import Mesh
from jax.sharding import PartitionSpec as P

DP = ("dp_0", "dp_1", "dp_2")
DP_MP = ("dp_0", "dp_1", "dp_2", "mp")
adam_count = 100.0
learn_rate = 0.05
decay_rate = 0.01


def sent_together(arrays, axis, dim, along):
    both = jnp.concatenate(arrays, axis=along)
    result, at, outs = (lax.all_gather(both, axis, axis=dim, tiled=True), 0, [])
    for a in arrays:
        outs.append(lax.slice_in_dim(result, at, at + a.shape[along], axis=along))
        at += a.shape[along]
    return tuple(outs)


def sent_together_2(arrays, axis, dim, along):
    ends, at = ([], 0)
    for a in arrays[:-1]:
        at += a.shape[along]
        ends.append(at)
    both = jnp.concatenate(arrays, axis=along)
    return tuple(
        jnp.split(lax.psum_scatter(both, axis, scatter_dimension=dim, tiled=True), ends, axis=along)
    )


def by_axis(shard, axes):
    return functools.reduce(lax.psum, axes, shard)


def gelu_pair(preact):
    tanh_arg = 0.7978845608028654 * (preact + 0.044715 * preact * preact * preact)
    tanh_val = jnp.tanh(tanh_arg)
    activation = 0.5 * preact * (1.0 + tanh_val)
    slopes = 0.5 * (1.0 + tanh_val) + 0.5 * preact * (
        1.0 - tanh_val * tanh_val
    ) * 0.7978845608028654 * (1.0 + 3.0 * 0.044715 * preact * preact)
    return (activation, slopes)


def distill_target(clean, noise, teacher_first, teacher_second, step_index, teacher_count):
    steps_float = teacher_count.astype(jnp.float32)[:, None, None]
    doubled = 2.0 * step_index.astype(jnp.float32)[:, None, None]
    quarter_turn = 0.5 * math.pi
    time_now = doubled / steps_float
    time_mid = (doubled - 1.0) / steps_float
    time_end = (doubled - 2.0) / steps_float
    alpha_now = jnp.cos(quarter_turn * time_now)
    sigma_now = jnp.sin(quarter_turn * time_now)
    alpha_mid = jnp.cos(quarter_turn * time_mid)
    sigma_mid = jnp.sin(quarter_turn * time_mid)
    alpha_end = jnp.cos(quarter_turn * time_end)
    sigma_end = jnp.sin(quarter_turn * time_end)
    first_f = teacher_first.astype(jnp.float32)
    second_f = teacher_second.astype(jnp.float32)
    latent_now = alpha_now * clean.astype(jnp.float32) + sigma_now * noise.astype(jnp.float32)
    noise_now = (latent_now - alpha_now * first_f) / sigma_now
    latent_mid = alpha_mid * first_f + sigma_mid * noise_now
    noise_mid = (latent_mid - alpha_mid * second_f) / sigma_mid
    latent_end = alpha_end * second_f + sigma_end * noise_mid
    sigma_ratio = sigma_end / sigma_now
    target = (latent_end - sigma_ratio * latent_now) / (alpha_end - sigma_ratio * alpha_now)
    weighting = jnp.maximum(alpha_now * alpha_now / (sigma_now * sigma_now), 1.0)[:, 0, 0]
    return (latent_now, target, weighting)


def adam_update(master, moment, second, gradient, factor):
    clipped = gradient * factor
    moment_new = 0.9 * moment + 0.1 * clipped
    second_new = 0.999 * second + 0.001 * clipped * clipped
    first_hat = moment_new / (1.0 - 0.9**adam_count)
    second_hat = second_new / (1.0 - 0.999**adam_count)
    master_new = master - learn_rate * (
        first_hat / (jnp.sqrt(second_hat) + 1e-08) + decay_rate * master
    )
    return (master_new, moment_new, second_new)


def per_device(
    clean,
    noise,
    teacher_first,
    teacher_second,
    step_index,
    teacher_count,
    up_master,
    down_master,
    up_moment,
    down_moment,
    up_second,
    down_second,
):
    samples_dev, token_count, width_local = clean.shape
    sample_total = samples_dev * lax.axis_size(DP)
    row_count = samples_dev * token_count
    latent, target, weighting = distill_target(
        clean, noise, teacher_first, teacher_second, step_index, teacher_count
    )
    noisy_rows = latent.reshape(row_count, width_local).astype(jnp.bfloat16)
    gathered = lax.all_gather(noisy_rows, "mp", axis=1, tiled=True)
    gathered_f = gathered.astype(jnp.float32)
    normed = (
        gathered_f * lax.rsqrt(jnp.mean(gathered_f * gathered_f, axis=1, keepdims=True) + 1e-06)
    ).astype(jnp.bfloat16)
    up_full, down_full = sent_together(
        (up_master.astype(jnp.bfloat16), down_master.astype(jnp.bfloat16)), DP, 0, 1
    )
    width_full = up_full.shape[0]
    hidden_local = up_full.shape[1]
    dscale = width_full ** (-0.5)
    fscale = (hidden_local * lax.axis_size("mp")) ** (-0.5)
    preact = jnp.dot(normed, up_full, preferred_element_type=jnp.float32) * dscale
    activation, slopes = gelu_pair(preact)
    hidden = activation.astype(jnp.bfloat16)
    partial_value = (
        lax.dot_general(
            hidden, down_full, (((1,), (1,)), ((), ())), preferred_element_type=jnp.float32
        )
        * fscale
    )
    branch = lax.psum_scatter(
        partial_value.astype(jnp.bfloat16), "mp", scatter_dimension=1, tiled=True
    ).astype(jnp.float32)
    errors = latent + branch.reshape(latent.shape) - target
    weight_cube = weighting[:, None, None]
    loss_part = jnp.sum(weight_cube * errors * errors)
    dpred = (
        (2.0 * weight_cube / sample_total * errors)
        .astype(jnp.bfloat16)
        .reshape(row_count, width_local)
    )
    piece = lax.all_gather(dpred, "mp", axis=1, tiled=True)
    summed = jnp.dot(piece, down_full, preferred_element_type=jnp.float32)
    grad_piece = (
        lax.dot_general(piece, hidden, (((0,), (0,)), ((), ())), preferred_element_type=jnp.float32)
        * fscale
    )
    dpre = (summed * fscale * slopes).astype(jnp.bfloat16)
    grad_up = (
        lax.dot_general(normed, dpre, (((0,), (0,)), ((), ())), preferred_element_type=jnp.float32)
        * dscale
    )
    owned_up, owned_down = sent_together_2((grad_up, grad_piece), DP, 0, 1)
    squares = jnp.sum(owned_up * owned_up) + jnp.sum(owned_down * owned_down)
    loss_total, square_total = (by_axis(loss_part, DP_MP), by_axis(squares, DP_MP))
    clip_limit = math.sqrt(2.0 * width_full * hidden_local * lax.axis_size("mp"))
    factor = clip_limit / jnp.maximum(jnp.sqrt(square_total), clip_limit)
    new_up, up_m, up_v = adam_update(up_master, up_moment, up_second, owned_up, factor)
    new_down, down_m, down_v = adam_update(
        down_master, down_moment, down_second, owned_down, factor
    )
    loss_mean = loss_total / (sample_total * token_count * width_full)
    return (new_up, new_down, up_m, down_m, up_v, down_v, loss_mean)


def solution(mesh):
    split = Mesh(mesh.devices.reshape(4, 4, 2, mesh.shape["mp"]), ("dp_0", "dp_1", "dp_2", "mp"))
    placed = (
        P(DP, None, "mp"),
        P(DP, None, "mp"),
        P(DP, None, "mp"),
        P(DP, None, "mp"),
        P(DP),
        P(DP),
        P(DP, "mp"),
        P(DP, "mp"),
        P(DP, "mp"),
        P(DP, "mp"),
        P(DP, "mp"),
        P(DP, "mp"),
    )
    return jax.shard_map(
        per_device,
        mesh=split,
        in_specs=placed,
        out_specs=(
            P(DP, "mp"),
            P(DP, "mp"),
            P(DP, "mp"),
            P(DP, "mp"),
            P(DP, "mp"),
            P(DP, "mp"),
            P(),
        ),
        check_vma=False,
    )
```

profile of v0, /device:TPU:2, one launch (start us, length us, event | category | flops | bytes accessed | tf_op | source)
XLA Modules:
  0.0 404.3 jit_solution(1169654670336712328)
XLA Ops:
  7.2 0.0 all-gather.4.cloned.1.call-start
  7.2 0.7 fusion.39
  8.0 1.3 fusion.27
  9.3 0.8 copy.76
  10.2 0.0 all-gather.4.cloned.1.call-update
  10.2 0.0 all-gather.6.cloned.1.call-start
  10.2 0.9 convert_element_type.57
  11.2 0.9 convert_element_type.58
  12.1 0.7 pad_maximum_fusion.1
  12.7 0.0 all-gather.6.cloned.1.call-update
  12.8 0.0 reduce-scatter.5.cloned.1.call-start
  12.8 45.4 %all-gather.4.cloned.1.call-done = bf16[1024,1536]{0,1:T(8,128)(2,1)} async-done(((bf16[1024,192]{0,1:T(8,128)(2,1)}), bf16[1024,1536]{0,1:T(8,128)(2,1)}) %all-gather.4.cloned.1.call-update) | async-done | bytes 3145744 | tf_op jit(solution)/shard_map/all_gather | solution.py:109
  58.3 0.0 copy-start
  58.3 2.7 fusion
  61.0 50.3 %all-gather.6.cloned.1.call-done = bf16[1536,1536]{1,0:T(8,128)(2,1)} async-done(((bf16[48,1536]{1,0:T(8,128)(2,1)}), bf16[1536,1536]{1,0:T(8,128)(2,1)}) %all-gather.6.cloned.1.call-update) | async-done | bytes 4718608 | tf_op jit(solution)/shard_map/all_gather | solution.py:18
  111.3 0.0 copy-done
  111.3 0.0 copy-start.12
  111.3 4.6 %fusion.6 = f32[1024,768]{1,0:T(8,128)S(1)} fusion(bf16[1024,1536]{0,1:T(8,128)(2,1)S(1)} %copy-done, f32[1024]{0:T(1024)S(1)} %add_rsqrt_fusion, bf16[1536,1536]{1,0:T(8,128)(2,1)} %all-gather.6.cloned.1.call-done), kind=kOutput, calls=%fused_computation.14 | convolution fusion | flops 2420637696 | bytes 8654848 | tf_op jit(solution)/shard_map/dot_general | solution.py:121
  115.9 0.0 copy-start.14
  115.9 1.8 copy-done.14
  117.7 0.0 copy-done.12
  117.7 4.4 %multiply_convert_fusion = bf16[1024,1536]{0,1:T(8,128)(2,1)} fusion(bf16[1536,1536]{1,0:T(8,128)(2,1)S(1)} %copy-done.12, f32[1024,768]{1,0:T(8,128)S(1)} %fusion.6), kind=kOutput, calls=%fused_computation.5 | convolution fusion | flops 2426929152 | bytes 8650752 | tf_op jit(solution)/shard_map/dot_general | solution.py:125
  122.1 0.0 copy-start.2
  122.1 0.0 copy-start.3
  122.1 0.0 copy-start.6
  122.1 0.0 copy-start.7
  122.1 0.0 reduce-scatter.5.cloned.1.call-update
  122.1 0.0 all-gather.8.cloned.1.call-start
  122.2 46.7 %reduce-scatter.5.cloned.1.call-done = bf16[1024,192]{0,1:T(8,128)(2,1)} async-done(((bf16[1024,1536]{0,1:T(8,128)(2,1)}), bf16[1024,192]{0,1:T(8,128)(2,1)}) %reduce-scatter.5.cloned.1.call-update) | async-done | bytes 393232 | tf_op jit(solution)/shard_map/reduce_scatter | solution.py:130
  169.0 1.1 reshape.70
  170.1 0.0 copy-done.2
  170.1 0.0 copy-done.3
  170.1 0.0 copy-done.6
  170.1 0.0 copy-done.7
  170.1 1.5 fusion.25
  171.6 0.1 fusion.28
  171.7 0.8 copy.77
  172.5 0.0 all-gather.8.cloned.1.call-update
  172.5 0.2 reduce-scatter.7.cloned.1.call-start
  172.8 44.4 %all-gather.8.cloned.1.call-done = bf16[1024,1536]{0,1:T(8,128)(2,1)} async-done(((bf16[1024,192]{0,1:T(8,128)(2,1)}), bf16[1024,1536]{0,1:T(8,128)(2,1)}) %all-gather.8.cloned.1.call-update) | async-done | bytes 3145744 | tf_op jit(solution)/shard_map/all_gather | solution.py:141
  217.2 8.1 %multiply_convert_fusion.1 = bf16[1024,768]{1,0:T(8,128)(2,1)S(1)} fusion(f32[1024,768]{1,0:T(8,128)} %copy-done.14, bf16[1024,1536]{0,1:T(8,128)(2,1)} %all-gather.8.cloned.1.call-done, bf16[1536,1536]{1,0:T(8,128)(2,1)} %all-gather.6.cloned.1.call-done), kind=kOutput, calls=%fused_computation.11 | convolution fusion | flops 2432434176 | bytes 10223616 | tf_op jit(solution)/shard_map/dot_general | solution.py:142
  225.3 0.0 copy-done.13
  225.3 0.0 copy-start.1
  225.3 5.2 %convolution_multiply_fusion = f32[1536,768]{0,1:T(8,128)S(1)} fusion(bf16[1024,1536]{0,1:T(8,128)(2,1)S(1)} %copy-done.13, f32[1024,768]{1,0:T(8,128)} %copy-done.14), kind=kOutput, calls=%fused_computation.7 | convolution fusion | flops 2424963072 | bytes 11010048 | tf_op jit(solution)/shard_map/dot_general | solution.py:144
  230.5 0.0 copy-done.1
  230.5 2.8 convolution_multiply_fusion.1
  233.3 4.5 %pad_maximum_fusion = f32[1536,1536]{0,1:T(8,128)} fusion(f32[1536,768]{0,1:T(8,128)S(1)} %convolution_multiply_fusion, f32[1536,768]{0,1:T(8,128)S(1)} %convolution_multiply_fusion.1), kind=kLoop, calls=%fused_computation | loop fusion | flops 2359296 | bytes 18874368 | tf_op jit(solution)/shard_map/concatenate | solution.py:30
  237.8 9.6 %copy.73 = f32[1536,1536]{1,0:T(8,128)} copy(f32[1536,1536]{0,1:T(8,128)} %pad_maximum_fusion) | data formatting | bytes 18874368
  247.5 0.0 copy-start.10
  247.5 0.0 copy-start.11
  247.5 0.0 reduce-scatter.7.cloned.1.call-update
  247.5 101.6 %reduce-scatter.7.cloned.1.call-done = f32[48,1536]{1,0:T(8,128)} async-done(((f32[1536,1536]{1,0:T(8,128)}), f32[48,1536]{1,0:T(8,128)}) %reduce-scatter.7.cloned.1.call-update) | async-done | bytes 294928 | tf_op jit(solution)/shard_map/reduce_scatter | solution.py:32
  349.1 1.6 multiply_reduce_fusion
  352.0 9.9 %all-reduce.2 = (f32[]{:T(128)}, f32[]{:T(128)}) all-reduce(f32[]{:T(128)S(6)} %add.97, f32[]{:T(128)} %get-tuple-element.44), channel_id=1, replica_groups=mesh['dp_0'=4,'dp_1'=4,'dp_2'=2,'mp'=8] {'dp_0'}, use_global_device_ids=true, to_apply=%region_5.0 | all-reduce | flops 2 | bytes 16 | tf_op jit(solution)/shard_map/psum | solution.py:37
  361.9 10.1 %all-reduce.1 = (f32[]{:T(128)}, f32[]{:T(128)}) all-reduce(f32[]{:T(128)} %get-tuple-element.34, f32[]{:T(128)} %get-tuple-element.35), channel_id=1, replica_groups=mesh['dp_0'=4,'dp_1'=4,'dp_2'=2,'mp'=8] {'dp_1'}, use_global_device_ids=true, to_apply=%region_6.0 | all-reduce | flops 2 | bytes 16 | tf_op jit(solution)/shard_map/psum | solution.py:37
  372.0 3.1 all-reduce.3
  375.1 18.1 %all-reduce = (f32[]{:T(128)}, f32[]{:T(128)}) all-reduce(f32[]{:T(128)} %get-tuple-element.36, f32[]{:T(128)} %get-tuple-element.37), channel_id=1, replica_groups=mesh['dp_0'=4,'dp_1'=4,'dp_2'=2,'mp'=8] {'mp'}, use_global_device_ids=true, to_apply=%region_8.0 | all-reduce | flops 2 | bytes 16 | tf_op jit(solution)/shard_map/psum | solution.py:37
  394.5 0.0 copy-done.4
  394.5 0.0 copy-done.5
  394.5 0.0 copy-done.8
  394.6 0.0 copy-done.9
  394.6 0.0 copy-done.10
  394.6 0.0 copy-done.11
  394.6 2.0 multiply_subtract_fusion
  (10 shorter events, 0.1 us)
Async XLA Ops:
  7.2 51.1 %all-gather.4.cloned.1.call-start = ((), (), s32[]{:S(2)}) async-start(), calls=%async_computation.2 | async-start | bytes 3538944 | tf_op jit(solution)/shard_map/all_gather | solution.py:109
  10.2 101.2 %all-gather.6.cloned.1.call-start = ((), (), s32[]{:S(2)}) async-start(), calls=%async_computation.3 | async-start | bytes 4866048 | tf_op jit(solution)/shard_map/all_gather | solution.py:18
  12.8 156.2 %reduce-scatter.5.cloned.1.call-start = ((), (), s32[]{:S(2)}) async-start(), calls=%async_computation.4 | async-start | bytes 3538944 | tf_op jit(solution)/shard_map/reduce_scatter | solution.py:130
  58.3 53.1 %copy-start = (bf16[1024,1536]{0,1:T(8,128)(2,1)S(1)}, bf16[1024,1536]{0,1:T(8,128)(2,1)}, u32[]{:S(2)}) copy-start(bf16[1024,1536]{0,1:T(8,128)(2,1)} %all-gather.4.cloned.1.call-done) | copy-start | bytes 9437188
  111.3 6.4 %copy-start.12 = (bf16[1536,1536]{1,0:T(8,128)(2,1)S(1)}, bf16[1536,1536]{1,0:T(8,128)(2,1)}, u32[]{:S(2)}) copy-start(bf16[1536,1536]{1,0:T(8,128)(2,1)} %all-gather.6.cloned.1.call-done) | copy-start | bytes 14155780
  115.9 1.8 copy-start.14
  122.1 48.0 %copy-start.2 = (bf16[4,256,192]{1,2,0:T(8,128)(2,1)S(1)}, bf16[4,256,192]{1,2,0:T(8,128)(2,1)}, u32[]{:S(2)}) copy-start(bf16[4,256,192]{1,2,0:T(8,128)(2,1)} %param.13) | copy-start | bytes 1179652
  122.1 48.0 %copy-start.3 = (bf16[4,256,192]{1,2,0:T(8,128)(2,1)S(1)}, bf16[4,256,192]{1,2,0:T(8,128)(2,1)}, u32[]{:S(2)}) copy-start(bf16[4,256,192]{1,2,0:T(8,128)(2,1)} %param.12) | copy-start | bytes 1179652
  122.1 48.0 %copy-start.6 = (bf16[4,256,192]{1,2,0:T(8,128)(2,1)S(1)}, bf16[4,256,192]{1,2,0:T(8,128)(2,1)}, u32[]{:S(2)}) copy-start(bf16[4,256,192]{1,2,0:T(8,128)(2,1)} %param.14) | copy-start | bytes 1179652
  122.1 48.0 %copy-start.7 = (bf16[4,256,192]{1,2,0:T(8,128)(2,1)S(1)}, bf16[4,256,192]{1,2,0:T(8,128)(2,1)}, u32[]{:S(2)}) copy-start(bf16[4,256,192]{1,2,0:T(8,128)(2,1)} %param.15) | copy-start | bytes 1179652
  122.1 95.1 %all-gather.8.cloned.1.call-start = ((), (), s32[]{:S(2)}) async-start(), calls=%async_computation.5 | async-start | bytes 3538944 | tf_op jit(solution)/shard_map/all_gather | solution.py:141
  172.5 176.6 %reduce-scatter.7.cloned.1.call-start = ((), (), s32[]{:S(2)}) async-start(), calls=%async_computation.6 | async-start | bytes 9732096 | tf_op jit(solution)/shard_map/reduce_scatter | solution.py:32
  217.2 8.1 %copy-start.13 = (bf16[1024,1536]{0,1:T(8,128)(2,1)S(1)}, bf16[1024,1536]{0,1:T(8,128)(2,1)}, u32[]{:S(2)}) copy-start(bf16[1024,1536]{0,1:T(8,128)(2,1)} %all-gather.8.cloned.1.call-done) | copy-start | bytes 9437188
  225.3 5.2 %copy-start.1 = (bf16[1024,1536]{0,1:T(8,128)(2,1)S(1)}, bf16[1024,1536]{0,1:T(8,128)(2,1)}, u32[]{:S(2)}) copy-start(bf16[1024,1536]{0,1:T(8,128)(2,1)} %all-gather.4.cloned.1.call-done) | copy-start | bytes 9437188
  247.5 147.1 %copy-start.4 = (f32[48,768]{1,0:T(8,128)S(1)}, f32[48,768]{1,0:T(8,128)}, u32[]{:S(2)}) copy-start(f32[48,768]{1,0:T(8,128)} %param.19) | copy-start | bytes 442372
  247.5 147.1 %copy-start.5 = (f32[48,768]{1,0:T(8,128)S(1)}, f32[48,768]{1,0:T(8,128)}, u32[]{:S(2)}) copy-start(f32[48,768]{1,0:T(8,128)} %param.18) | copy-start | bytes 442372
  247.5 147.1 %copy-start.8 = (f32[48,768]{1,0:T(8,128)S(1)}, f32[48,768]{1,0:T(8,128)}, u32[]{:S(2)}) copy-start(f32[48,768]{1,0:T(8,128)} %param.21) | copy-start | bytes 442372
  247.5 147.1 %copy-start.9 = (f32[48,768]{1,0:T(8,128)S(1)}, f32[48,768]{1,0:T(8,128)}, u32[]{:S(2)}) copy-start(f32[48,768]{1,0:T(8,128)} %param.23) | copy-start | bytes 442372
  247.5 147.1 %copy-start.10 = (f32[48,768]{1,0:T(8,128)S(1)}, f32[48,768]{1,0:T(8,128)}, u32[]{:S(2)}) copy-start(f32[48,768]{1,0:T(8,128)} %param.22) | copy-start | bytes 442372
  247.5 147.1 %copy-start.11 = (f32[48,768]{1,0:T(8,128)S(1)}, f32[48,768]{1,0:T(8,128)}, u32[]{:S(2)}) copy-start(f32[48,768]{1,0:T(8,128)} %param.20) | copy-start | bytes 442372
Sparse Core Ops, SparseCore 0:
  10.3 47.9 all-gather.3
  61.4 49.9 all-gather.5
  122.2 46.7 reduce-scatter.4
  172.6 44.4 all-gather.7
  247.6 101.4 reduce-scatter.6
where the time goes:
time: 405 us; the launch traced here: 404 us
  waiting for transfers between devices  289 us (71%)
  blocking collectives  41.1 us (10%)
  matrix products  25 us (6%)
  other arithmetic  18.2 us (4%)
  between operations  17.8 us (4%)
  local copies, waits for them, and re-layouts  13.2 us (3%)
    reduce_scatter x1, waiting for transfers between devices, sent_together_2(): lax.psum_scatter(both, axis, scatter_dimension=dim, tiled=True)  102 us
    all_gather x1, waiting for transfers between devices, sent_together(): result, at, outs = (lax.all_gather(both, axis, axis=dim, tiled=True), 0, [])  50.3 us
    reduce_scatter x1, waiting for transfers between devices, per_device(): lax.psum_scatter(partial_value.astype(jnp.bfloat16), 'mp', scatter_dimens...  46.7 us
    all_gather x1, waiting for transfers between devices, per_device(): gathered = lax.all_gather(noisy_rows, 'mp', axis=1, tiled=True)  45.4 us
    all_gather x1, waiting for transfers between devices, per_device(): piece = lax.all_gather(dpred, 'mp', axis=1, tiled=True)  44.4 us
    psum x4, blocking collectives, by_axis(): return functools.reduce(lax.psum, axes, shard)  41.1 us
    unnamed x31, local copies, waits for them, and re-layouts  11.5 us
  transfers between devices with their start and end apart: 5, of which 5 were waited for; matrix products, arithmetic and copies ran while one was open for 1% of the time, Pallas kernels for 0%

commit v1 on v0

--- a/solution.py
+++ b/solution.py
@@ -11,6 +11,18 @@
 adam_count = 100.0
 learn_rate = 0.05
 decay_rate = 0.01
+
+
+def gather_around(array, axis, dim):
+    ways, here, step = (lax.axis_size(axis), lax.axis_index(axis), array.shape[dim])
+    lengths = [n * ways if d == dim else n for d, n in enumerate(array.shape)]
+    full = lax.dynamic_update_slice_in_dim(
+        jnp.zeros(lengths, array.dtype), array, here * step, axis=dim
+    )
+    for far in range(1, ways):
+        array = lax.ppermute(array, axis, [(d, (d + 1) % ways) for d in range(ways)])
+        full = lax.dynamic_update_slice_in_dim(full, array, (here - far) % ways * step, axis=dim)
+    return full
 
 
 def sent_together(arrays, axis, dim, along):
@@ -138,7 +150,7 @@
         .astype(jnp.bfloat16)
         .reshape(row_count, width_local)
     )
-    piece = lax.all_gather(dpred, "mp", axis=1, tiled=True)
+    piece = gather_around(dpred, "mp", 1)
     summed = jnp.dot(piece, down_full, preferred_element_type=jnp.float32)
     grad_piece = (
         lax.dot_general(piece, hidden, (((0,), (0,)), ((), ())), preferred_element_type=jnp.float32)

time: 405 us -> 433 us (1.069)
  waiting for transfers between devices: 289 us -> 320 us
  matrix products: 25 us -> 19.4 us
    ppermute x0 -> x7, waiting for transfers between devices: none -> 74.2 us  [gather_around(): lax.ppermute(array, axis, [(d, (d + 1) % ways) for d in range(ways)])]
    all_gather x1 -> x0, waiting for transfers between devices: 44.4 us -> none  [per_device(): piece = lax.all_gather(dpred, 'mp', axis=1, tiled=True)]
    unnamed x31 -> x41, local copies, waits for them, and re-layouts: 11.5 us -> 12 us
  transfers between devices with their start and end apart: 5 -> 11, of which waited for: 5 -> 11; matrix products, arithmetic and copies ran while one was open for 1% -> 1% of each run, Pallas kernels for 0% -> 0%
where the time goes in v1:
time: 433 us
  waiting for transfers between devices  320 us (74%)
  blocking collectives  41.1 us (9%)
  matrix products  19.4 us (4%)
  other arithmetic  18.7 us (4%)
  between operations  18 us (4%)
  local copies, waits for them, and re-layouts  13.7 us (3%)
    reduce_scatter x1, waiting for transfers between devices, sent_together_2(): lax.psum_scatter(both, axis, scatter_dimension=dim, tiled=True)  103 us
    ppermute x7, waiting for transfers between devices, gather_around(): lax.ppermute(array, axis, [(d, (d + 1) % ways) for d in range(ways)])  74.2 us
    all_gather x1, waiting for transfers between devices, sent_together(): result, at, outs = (lax.all_gather(both, axis, axis=dim, tiled=True), 0, [])  50.3 us
    reduce_scatter x1, waiting for transfers between devices, per_device(): lax.psum_scatter(partial_value.astype(jnp.bfloat16), 'mp', scatter_dimens...  46.3 us
    all_gather x1, waiting for transfers between devices, per_device(): gathered = lax.all_gather(noisy_rows, 'mp', axis=1, tiled=True)  45.4 us
    psum x4, blocking collectives, by_axis(): return functools.reduce(lax.psum, axes, shard)  41.1 us
    unnamed x41, local copies, waits for them, and re-layouts  12 us
  transfers between devices with their start and end apart: 11, of which 11 were waited for; matrix products, arithmetic and copies ran while one was open for 1% of the time, Pallas kernels for 0%

profile of v1, /device:TPU:2, one launch (start us, length us, event | category | flops | bytes accessed | tf_op | source)
XLA Modules:
  0.0 433.0 jit_solution(5566452543630471601)
XLA Ops:
  7.2 0.0 all-gather.3.cloned.1.call-start
  7.2 1.2 fusion.39
  8.5 1.3 fusion.27
  9.8 0.8 copy.76
  10.7 0.0 all-gather.3.cloned.1.call-update
  10.7 0.0 all-gather.5.cloned.1.call-start
  10.8 0.9 convert_element_type.57
  11.7 0.9 convert_element_type.58
  12.6 0.7 pad_maximum_fusion.1
  13.3 0.0 all-gather.5.cloned.1.call-update
  13.3 0.0 reduce-scatter.5.cloned.1.call-start
  13.4 45.4 %all-gather.3.cloned.1.call-done = bf16[1024,1536]{0,1:T(8,128)(2,1)} async-done(((bf16[1024,192]{0,1:T(8,128)(2,1)}), bf16[1024,1536]{0,1:T(8,128)(2,1)}) %all-gather.3.cloned.1.call-update) | async-done | bytes 3145744 | tf_op jit(solution)/shard_map/all_gather | solution.py:121
  58.8 2.7 fusion
  61.6 50.3 %all-gather.5.cloned.1.call-done = bf16[1536,1536]{1,0:T(8,128)(2,1)} async-done(((bf16[48,1536]{1,0:T(8,128)(2,1)}), bf16[1536,1536]{1,0:T(8,128)(2,1)}) %all-gather.5.cloned.1.call-update) | async-done | bytes 4718608 | tf_op jit(solution)/shard_map/all_gather | solution.py:30
  111.9 4.6 %fusion.6 = f32[1024,768]{1,0:T(8,128)S(1)} fusion(bf16[1024,1536]{0,1:T(8,128)(2,1)S(1)} %copy-done, f32[1024]{0:T(1024)S(1)} %add_rsqrt_fusion, bf16[1536,1536]{1,0:T(8,128)(2,1)} %all-gather.5.cloned.1.call-done), kind=kOutput, calls=%fused_computation.14 | convolution fusion | flops 2420637696 | bytes 8654848 | tf_op jit(solution)/shard_map/dot_general | solution.py:133
  116.5 1.7 copy-done.16
  118.2 4.4 %multiply_convert_fusion = bf16[1024,1536]{0,1:T(8,128)(2,1)} fusion(bf16[1536,1536]{1,0:T(8,128)(2,1)S(1)} %copy-done.15, f32[1024,768]{1,0:T(8,128)S(1)} %fusion.6), kind=kOutput, calls=%fused_computation.5 | convolution fusion | flops 2426929152 | bytes 8650752 | tf_op jit(solution)/shard_map/dot_general | solution.py:137
  122.6 0.0 copy-start.6
  122.6 0.0 copy-start.7
  122.6 0.0 copy-start.12
  122.6 0.0 reduce-scatter.5.cloned.1.call-update
  122.7 0.0 reduce-scatter.7.cloned.1.call-start
  122.7 0.5 copy-done.14
  123.3 46.3 %reduce-scatter.5.cloned.1.call-done = bf16[1024,192]{0,1:T(8,128)(2,1)} async-done(((bf16[1024,1536]{0,1:T(8,128)(2,1)}), bf16[1024,192]{0,1:T(8,128)(2,1)}) %reduce-scatter.5.cloned.1.call-update) | async-done | bytes 393232 | tf_op jit(solution)/shard_map/reduce_scatter | solution.py:142
  169.6 1.1 reshape.70
  170.7 0.0 copy-done.2
  170.7 0.0 copy-done.3
  170.7 0.0 copy-done.6
  170.7 0.0 copy-done.7
  170.7 0.0 copy-done.12
  170.7 1.5 fusion.25
  172.2 0.1 fusion.28
  172.4 0.8 collective-permute-start
  173.2 8.6 %collective-permute-done = bf16[1024,192]{0,1:T(8,128)(2,1)S(1)} collective-permute-done((bf16[1024,192]{0,1:T(8,128)(2,1)S(1)}, bf16[1024,192]{0,1:T(8,128)(2,1)S(1)}, u32[]{:S(2)}, u32[]{:S(2)}) %collective-permute-start) | collective-permute-done | bytes 393248 | tf_op jit(solution)/shard_map/ppermute | solution.py:23
  181.8 0.1 collective-permute-start.1
  181.9 10.3 %collective-permute-done.1 = bf16[1024,192]{0,1:T(8,128)(2,1)S(1)} collective-permute-done((bf16[1024,192]{0,1:T(8,128)(2,1)S(1)}, bf16[1024,192]{0,1:T(8,128)(2,1)S(1)}, u32[]{:S(2)}, u32[]{:S(2)}) %collective-permute-start.1) | collective-permute-done | bytes 393248 | tf_op jit(solution)/shard_map/ppermute | solution.py:23
  192.2 0.5 collective-permute-start.2
  192.6 11.1 %collective-permute-done.2 = bf16[1024,192]{0,1:T(8,128)(2,1)S(1)} collective-permute-done((bf16[1024,192]{0,1:T(8,128)(2,1)S(1)}, bf16[1024,192]{0,1:T(8,128)(2,1)S(1)}, u32[]{:S(2)}, u32[]{:S(2)}) %collective-permute-start.2) | collective-permute-done | bytes 393248 | tf_op jit(solution)/shard_map/ppermute | solution.py:23
  203.7 0.8 collective-permute-start.3
  204.5 11.9 %collective-permute-done.3 = bf16[1024,192]{0,1:T(8,128)(2,1)S(1)} collective-permute-done((bf16[1024,192]{0,1:T(8,128)(2,1)S(1)}, bf16[1024,192]{0,1:T(8,128)(2,1)S(1)}, u32[]{:S(2)}, u32[]{:S(2)}) %collective-permute-start.3) | collective-permute-done | bytes 393248 | tf_op jit(solution)/shard_map/ppermute | solution.py:23
  216.4 0.1 collective-permute-start.4
  216.5 12.5 %collective-permute-done.4 = bf16[1024,192]{0,1:T(8,128)(2,1)S(1)} collective-permute-done((bf16[1024,192]{0,1:T(8,128)(2,1)S(1)}, bf16[1024,192]{0,1:T(8,128)(2,1)S(1)}, u32[]{:S(2)}, u32[]{:S(2)}) %collective-permute-start.4) | collective-permute-done | bytes 393248 | tf_op jit(solution)/shard_map/ppermute | solution.py:23
  228.9 0.0 collective-permute-start.5
  228.9 0.4 broadcast_in_dim.2
  229.5 11.2 %collective-permute-done.5 = bf16[1024,192]{0,1:T(8,128)(2,1)S(1)} collective-permute-done((bf16[1024,192]{0,1:T(8,128)(2,1)S(1)}, bf16[1024,192]{0,1:T(8,128)(2,1)S(1)}, u32[]{:S(2)}, u32[]{:S(2)}) %collective-permute-start.5) | collective-permute-done | bytes 393248 | tf_op jit(solution)/shard_map/ppermute | solution.py:23
  240.7 0.0 collective-permute-start.6
  240.8 0.0 slice-start
  240.8 8.8 %collective-permute-done.6 = bf16[1024,192]{0,1:T(8,128)(2,1)S(1)} collective-permute-done((bf16[1024,192]{0,1:T(8,128)(2,1)S(1)}, bf16[1024,192]{0,1:T(8,128)(2,1)S(1)}, u32[]{:S(2)}, u32[]{:S(2)}) %collective-permute-start.6) | collective-permute-done | bytes 393248 | tf_op jit(solution)/shard_map/ppermute | solution.py:23
  249.7 0.0 slice-start.1
  249.7 3.2 convolution_multiply_fusion
  252.9 4.5 %multiply_convert_fusion.1 = bf16[1024,768]{1,0:T(8,128)(2,1)S(1)} fusion(f32[1024,768]{1,0:T(8,128)S(1)} %copy-done.17, bf16[1024,1536]{0,1:T(8,128)(2,1)S(1)} %constant_dynamic-update-slice_fusion, bf16[1536,1536]{1,0:T(8,128)(2,1)S(1)} %bitcast.21), kind=kOutput, calls=%fused_computation.11 | convolution fusion | flops 2432434176 | bytes 10223616 | tf_op jit(solution)/shard_map/dot_general | solution.py:154
  257.5 2.8 convolution_multiply_fusion.1
  260.2 4.5 %pad_maximum_fusion = f32[1536,1536]{0,1:T(8,128)} fusion(f32[1536,768]{0,1:T(8,128)S(1)} %convolution_multiply_fusion, f32[1536,768]{0,1:T(8,128)S(1)} %convolution_multiply_fusion.1), kind=kLoop, calls=%fused_computation | loop fusion | flops 2359296 | bytes 18874368 | tf_op jit(solution)/shard_map/concatenate | solution.py:42
  264.8 9.7 %copy.73 = f32[1536,1536]{1,0:T(8,128)} copy(f32[1536,1536]{0,1:T(8,128)} %pad_maximum_fusion) | data formatting | bytes 18874368
  274.4 0.0 copy-start.10
  274.4 0.0 copy-start.11
  274.4 0.0 reduce-scatter.7.cloned.1.call-update
  274.5 103.4 %reduce-scatter.7.cloned.1.call-done = f32[48,1536]{1,0:T(8,128)} async-done(((f32[1536,1536]{1,0:T(8,128)}), f32[48,1536]{1,0:T(8,128)}) %reduce-scatter.7.cloned.1.call-update) | async-done | bytes 294928 | tf_op jit(solution)/shard_map/reduce_scatter | solution.py:44
  377.8 1.6 multiply_reduce_fusion
  380.8 9.9 %all-reduce.2 = (f32[]{:T(128)}, f32[]{:T(128)}) all-reduce(f32[]{:T(128)S(6)} %add.165, f32[]{:T(128)} %get-tuple-element.44), channel_id=1, replica_groups=mesh['dp_0'=4,'dp_1'=4,'dp_2'=2,'mp'=8] {'dp_0'}, use_global_device_ids=true, to_apply=%region_5.6 | all-reduce | flops 2 | bytes 16 | tf_op jit(solution)/shard_map/psum | solution.py:49
  390.6 10.1 %all-reduce.1 = (f32[]{:T(128)}, f32[]{:T(128)}) all-reduce(f32[]{:T(128)} %get-tuple-element.34, f32[]{:T(128)} %get-tuple-element.35), channel_id=1, replica_groups=mesh['dp_0'=4,'dp_1'=4,'dp_2'=2,'mp'=8] {'dp_1'}, use_global_device_ids=true, to_apply=%region_6.7 | all-reduce | flops 2 | bytes 16 | tf_op jit(solution)/shard_map/psum | solution.py:49
  400.7 3.1 all-reduce.3
  403.8 18.1 %all-reduce = (f32[]{:T(128)}, f32[]{:T(128)}) all-reduce(f32[]{:T(128)} %get-tuple-element.36, f32[]{:T(128)} %get-tuple-element.37), channel_id=1, replica_groups=mesh['dp_0'=4,'dp_1'=4,'dp_2'=2,'mp'=8] {'mp'}, use_global_device_ids=true, to_apply=%region_8.9 | all-reduce | flops 2 | bytes 16 | tf_op jit(solution)/shard_map/psum | solution.py:49
  423.3 2.0 multiply_subtract_fusion
  (41 shorter events, 0.5 us)
Async XLA Ops:
  7.2 51.6 %all-gather.3.cloned.1.call-start = ((), (), s32[]{:S(2)}) async-start(), calls=%async_computation.2 | async-start | bytes 3538944 | tf_op jit(solution)/shard_map/all_gather | solution.py:121
  10.7 101.2 %all-gather.5.cloned.1.call-start = ((), (), s32[]{:S(2)}) async-start(), calls=%async_computation.3 | async-start | bytes 4866048 | tf_op jit(solution)/shard_map/all_gather | solution.py:30
  13.3 156.3 %reduce-scatter.5.cloned.1.call-start = ((), (), s32[]{:S(2)}) async-start(), calls=%async_computation.4 | async-start | bytes 3538944 | tf_op jit(solution)/shard_map/reduce_scatter | solution.py:142
  58.8 53.1 %copy-start = (bf16[1024,1536]{0,1:T(8,128)(2,1)S(1)}, bf16[1024,1536]{0,1:T(8,128)(2,1)}, u32[]{:S(2)}) copy-start(bf16[1024,1536]{0,1:T(8,128)(2,1)} %all-gather.3.cloned.1.call-done) | copy-start | bytes 9437188
  111.9 6.3 %copy-start.15 = (bf16[1536,1536]{1,0:T(8,128)(2,1)S(1)}, bf16[1536,1536]{1,0:T(8,128)(2,1)}, u32[]{:S(2)}) copy-start(bf16[1536,1536]{1,0:T(8,128)(2,1)} %all-gather.5.cloned.1.call-done) | copy-start | bytes 14155780
  116.5 1.8 copy-start.16
  122.6 0.7 copy-start.14
  122.6 0.7 copy-start.13
  122.6 48.1 %copy-start.2 = (bf16[4,256,192]{1,2,0:T(8,128)(2,1)S(1)}, bf16[4,256,192]{1,2,0:T(8,128)(2,1)}, u32[]{:S(2)}) copy-start(bf16[4,256,192]{1,2,0:T(8,128)(2,1)} %param.13) | copy-start | bytes 1179652
  122.6 48.1 %copy-start.3 = (bf16[4,256,192]{1,2,0:T(8,128)(2,1)S(1)}, bf16[4,256,192]{1,2,0:T(8,128)(2,1)}, u32[]{:S(2)}) copy-start(bf16[4,256,192]{1,2,0:T(8,128)(2,1)} %param.12) | copy-start | bytes 1179652
  122.6 48.1 %copy-start.6 = (bf16[4,256,192]{1,2,0:T(8,128)(2,1)S(1)}, bf16[4,256,192]{1,2,0:T(8,128)(2,1)}, u32[]{:S(2)}) copy-start(bf16[4,256,192]{1,2,0:T(8,128)(2,1)} %param.14) | copy-start | bytes 1179652
  122.6 48.1 %copy-start.7 = (bf16[4,256,192]{1,2,0:T(8,128)(2,1)S(1)}, bf16[4,256,192]{1,2,0:T(8,128)(2,1)}, u32[]{:S(2)}) copy-start(bf16[4,256,192]{1,2,0:T(8,128)(2,1)} %param.15) | copy-start | bytes 1179652
  122.6 48.1 %copy-start.12 = (f32[4]{0:T(128)S(1)}, f32[4]{0:T(128)}, u32[]{:S(2)}) copy-start(f32[4]{0:T(128)} %get-tuple-element.48) | copy-start | bytes 52
  122.7 255.2 %reduce-scatter.7.cloned.1.call-start = ((), (), s32[]{:S(2)}) async-start(), calls=%async_computation.5 | async-start | bytes 9732096 | tf_op jit(solution)/shard_map/reduce_scatter | solution.py:44
  172.4 9.4 %collective-permute-start = (bf16[1024,192]{0,1:T(8,128)(2,1)S(1)}, bf16[1024,192]{0,1:T(8,128)(2,1)S(1)}, u32[]{:S(2)}, u32[]{:S(2)}) collective-permute-start(bf16[1024,192]{0,1:T(8,128)(2,1)S(1)} %bitcast.18), channel_id=1, source_target_pairs={{0,1},{1,2},{2,3},{3,4},{4,5},{5,6},{6,7},{7,0},{8,9},{9,10},{10,1... | collective-permute-start | bytes 1179656 | tf_op jit(solution)/shard_map/ppermute | solution.py:23
  181.8 10.4 %collective-permute-start.1 = (bf16[1024,192]{0,1:T(8,128)(2,1)S(1)}, bf16[1024,192]{0,1:T(8,128)(2,1)S(1)}, u32[]{:S(2)}, u32[]{:S(2)}) collective-permute-start(bf16[1024,192]{0,1:T(8,128)(2,1)S(1)} %collective-permute-done), channel_id=1, source_target_pairs={{0,1},{1,2},{2,3},{3,4},{4,5},{5,6},{6,7},{7,0},{8,9},{9,10},{10,1... | collective-permute-start | bytes 1179656 | tf_op jit(solution)/shard_map/ppermute | solution.py:23
  192.2 11.5 %collective-permute-start.2 = (bf16[1024,192]{0,1:T(8,128)(2,1)S(1)}, bf16[1024,192]{0,1:T(8,128)(2,1)S(1)}, u32[]{:S(2)}, u32[]{:S(2)}) collective-permute-start(bf16[1024,192]{0,1:T(8,128)(2,1)S(1)} %collective-permute-done.1), channel_id=1, source_target_pairs={{0,1},{1,2},{2,3},{3,4},{4,5},{5,6},{6,7},{7,0},{8,9},{9,10},{10,1... | collective-permute-start | bytes 1179656 | tf_op jit(solution)/shard_map/ppermute | solution.py:23
  203.7 12.7 %collective-permute-start.3 = (bf16[1024,192]{0,1:T(8,128)(2,1)S(1)}, bf16[1024,192]{0,1:T(8,128)(2,1)S(1)}, u32[]{:S(2)}, u32[]{:S(2)}) collective-permute-start(bf16[1024,192]{0,1:T(8,128)(2,1)S(1)} %collective-permute-done.2), channel_id=1, source_target_pairs={{0,1},{1,2},{2,3},{3,4},{4,5},{5,6},{6,7},{7,0},{8,9},{9,10},{10,1... | collective-permute-start | bytes 1179656 | tf_op jit(solution)/shard_map/ppermute | solution.py:23
  216.4 12.6 %collective-permute-start.4 = (bf16[1024,192]{0,1:T(8,128)(2,1)S(1)}, bf16[1024,192]{0,1:T(8,128)(2,1)S(1)}, u32[]{:S(2)}, u32[]{:S(2)}) collective-permute-start(bf16[1024,192]{0,1:T(8,128)(2,1)S(1)} %collective-permute-done.3), channel_id=1, source_target_pairs={{0,1},{1,2},{2,3},{3,4},{4,5},{5,6},{6,7},{7,0},{8,9},{9,10},{10,1... | collective-permute-start | bytes 1179656 | tf_op jit(solution)/shard_map/ppermute | solution.py:23
  228.9 11.7 %collective-permute-start.5 = (bf16[1024,192]{0,1:T(8,128)(2,1)S(1)}, bf16[1024,192]{0,1:T(8,128)(2,1)S(1)}, u32[]{:S(2)}, u32[]{:S(2)}) collective-permute-start(bf16[1024,192]{0,1:T(8,128)(2,1)S(1)} %collective-permute-done.4), channel_id=1, source_target_pairs={{0,1},{1,2},{2,3},{3,4},{4,5},{5,6},{6,7},{7,0},{8,9},{9,10},{10,1... | collective-permute-start | bytes 1179656 | tf_op jit(solution)/shard_map/ppermute | solution.py:23
  229.3 20.3 %copy-start.17 = (f32[1024,768]{1,0:T(8,128)S(1)}, f32[1024,768]{1,0:T(8,128)}, u32[]{:S(2)}) copy-start(f32[1024,768]{1,0:T(8,128)} %copy-done.16) | copy-start | bytes 9437188
  240.7 9.0 %collective-permute-start.6 = (bf16[1024,192]{0,1:T(8,128)(2,1)S(1)}, bf16[1024,192]{0,1:T(8,128)(2,1)S(1)}, u32[]{:S(2)}, u32[]{:S(2)}) collective-permute-start(bf16[1024,192]{0,1:T(8,128)(2,1)S(1)} %collective-permute-done.5), channel_id=1, source_target_pairs={{0,1},{1,2},{2,3},{3,4},{4,5},{5,6},{6,7},{7,0},{8,9},{9,10},{10,1... | collective-permute-start | bytes 1179656 | tf_op jit(solution)/shard_map/ppermute | solution.py:23
  240.8 12.1 %slice-start = ((s8[4718592]{0:T(1024)(128)(4,1)}), s8[524288]{0:T(1024)(128)(4,1)S(1)}, s32[]{:S(2)}) async-start(s8[4718592]{0:T(1024)(128)(4,1)} %bitcast.20), calls=%async_computation.6 | async-start | bytes 1048576
  249.7 3.2 slice-start.1
  252.9 4.5 %copy-start.1 = (bf16[1024,1536]{0,1:T(8,128)(2,1)S(1)}, bf16[1024,1536]{0,1:T(8,128)(2,1)}, u32[]{:S(2)}) copy-start(bf16[1024,1536]{0,1:T(8,128)(2,1)} %all-gather.3.cloned.1.call-done) | copy-start | bytes 9437188
  274.4 148.8 %copy-start.4 = (f32[48,768]{1,0:T(8,128)S(1)}, f32[48,768]{1,0:T(8,128)}, u32[]{:S(2)}) copy-start(f32[48,768]{1,0:T(8,128)} %param.19) | copy-start | bytes 442372
  274.4 148.8 %copy-start.5 = (f32[48,768]{1,0:T(8,128)S(1)}, f32[48,768]{1,0:T(8,128)}, u32[]{:S(2)}) copy-start(f32[48,768]{1,0:T(8,128)} %param.18) | copy-start | bytes 442372
  274.4 148.8 %copy-start.8 = (f32[48,768]{1,0:T(8,128)S(1)}, f32[48,768]{1,0:T(8,128)}, u32[]{:S(2)}) copy-start(f32[48,768]{1,0:T(8,128)} %param.21) | copy-start | bytes 442372
  274.4 148.8 %copy-start.9 = (f32[48,768]{1,0:T(8,128)S(1)}, f32[48,768]{1,0:T(8,128)}, u32[]{:S(2)}) copy-start(f32[48,768]{1,0:T(8,128)} %param.23) | copy-start | bytes 442372
  274.4 148.8 %copy-start.10 = (f32[48,768]{1,0:T(8,128)S(1)}, f32[48,768]{1,0:T(8,128)}, u32[]{:S(2)}) copy-start(f32[48,768]{1,0:T(8,128)} %param.22) | copy-start | bytes 442372
  274.4 148.8 %copy-start.11 = (f32[48,768]{1,0:T(8,128)S(1)}, f32[48,768]{1,0:T(8,128)}, u32[]{:S(2)}) copy-start(f32[48,768]{1,0:T(8,128)} %param.20) | copy-start | bytes 442372
Sparse Core Ops, SparseCore 0:
  10.8 47.9 all-gather.2
  61.9 49.9 all-gather.4
  122.8 46.7 reduce-scatter.4
  274.6 103.1 reduce-scatter.6
